TPU v7x, 512 devices: a whole 4x4x16 slice. The times are simulated.
512 devices in a mesh: dp: 16 (over y_lo, x, core), ctx: 32 (over y_hi, z).
Axes of the slice: x: 4, y: 4 (y_hi: 2, y_lo: 2; y = y_hi * 2 + y_lo), z: 16, core: 2. Of those that a mesh axis runs over, the one named last changes fastest.
Arguments:
- grad_out: bfloat16 [65536, 4096], P(('dp', 'ctx')), may hold values from -24 to 24
- gate: bfloat16 [65536, 4096], P(('dp', 'ctx')), may hold values from -6 to 6
- conv_in: bfloat16 [65536, 4096], P(('dp', 'ctx')), may hold values from -6 to 6
- filt: bfloat16 [4096, 64], P('dp'), may hold values from -0.75 to 0.75
- doc_end: int32 [65536], P(('dp', 'ctx')), may hold values from 1 to 65536, as said below
Outputs:
- grad_in: bfloat16 [65536, 4096], P(('dp', 'ctx'))
- grad_filt: float32 [4096, 64], P('dp')
Inputs may be any that keep to these rules, and one draw needn't show every extreme that they name: doc_end is the same for all rows of one document and larger than the row's own index; no document crosses a multiple of 4096.
All inputs are finite; a program needn't handle non-finite values.
Results may differ from a plain program's by a relative error of at most 0.0049.
Values may be sent and summed in bfloat16 or wider, within the bound.
A program may use at most 64 MiB of HBM per device.

v0:
```python
import jax
import jax.numpy as jnp
from jax import lax
from jax.sharding import PartitionSpec as P


def from_behind(value, axis, steps):
    count = lax.axis_size(axis)
    first, last = (max(0, -steps), min(count, count - steps))
    return lax.ppermute(value, axis, [(source, source + steps) for source in range(first, last)])


def body(grad_out, gate, conv_in, filt, doc_end):
    row_count, channels = grad_out.shape
    tap_count = filt.shape[1]
    group_size = 8
    whole_filter = lax.all_gather(filt, "dp", axis=0, tiled=True)
    filter_rows = whole_filter.T
    grad_y = (grad_out.astype(jnp.float32) * gate.astype(jnp.float32)).astype(jnp.bfloat16)
    following = from_behind(grad_y, "ctx", -1)
    extended = jnp.concatenate([grad_y, following], axis=0)
    first_row = (lax.axis_index("dp") * lax.axis_size("ctx") + lax.axis_index("ctx")) * row_count
    remaining = doc_end - (first_row + jnp.arange(row_count, dtype=jnp.int32))
    within = jnp.arange(group_size, dtype=jnp.int32)

    def one_group(which, state):
        accum, tap_rows = state
        base = (which * group_size).astype(jnp.int32)
        offsets = base + within
        windows = jax.vmap(lambda offset: lax.dynamic_slice_in_dim(extended, offset, row_count, 0))(
            offsets
        )
        inside = (offsets[:, None] < remaining[None, :])[:, :, None]
        windows = jnp.where(inside, windows, jnp.zeros((), jnp.bfloat16))
        weights = lax.dynamic_slice_in_dim(filter_rows, base, group_size, 0)
        accum = accum + jnp.einsum(
            "trc,tc->rc", windows, weights, preferred_element_type=jnp.float32
        )
        tap_block = jnp.einsum("trc,rc->tc", windows, conv_in, preferred_element_type=jnp.float32)
        tap_rows = lax.dynamic_update_slice_in_dim(tap_rows, tap_block, base, 0)
        return (accum, tap_rows)

    start = (
        jnp.zeros((row_count, channels), jnp.float32),
        jnp.zeros((tap_count, channels), jnp.float32),
    )
    accum, tap_rows = lax.fori_loop(0, tap_count // group_size, one_group, start)
    grad_in = accum.astype(jnp.bfloat16)
    filt_terms = tap_rows.T
    owned = lax.psum_scatter(filt_terms, "dp", scatter_dimension=0, tiled=True)
    grad_filt = lax.psum(owned, "ctx")
    return (grad_in, grad_filt)


def solution(mesh):
    placed = (
        P(("dp", "ctx"), None),
        P(("dp", "ctx"), None),
        P(("dp", "ctx"), None),
        P("dp", None),
        P(("dp", "ctx")),
    )
    return jax.shard_map(
        body,
        mesh=mesh,
        in_specs=placed,
        out_specs=(P(("dp", "ctx"), None), P("dp", None)),
        check_vma=False,
    )
```

profile of v0, /device:TPU:2, one launch (start us, length us, event | category | flops | bytes accessed | tf_op | source)
XLA Modules:
  0.0 696.5 jit_solution(7880382249761035540)
XLA Ops:
  7.2 1.9 multiply_convert_fusion
  11.1 24.8 %all_gather.3 = bf16[4096,64]{0,1:T(8,128)(2,1)} all-gather(bf16[256,64]{0,1:T(8,128)(2,1)} %param.10), channel_id=1, replica_groups=mesh['dp'=16,'ctx'=32] {'dp'}, dimensions={0}, use_global_device_ids=true | all-gather | bytes 557056 | tf_op jit(solution)/shard_map/all_gather | solution.py:17
  39.0 302.4 %while.23 = (s32[]{:T(128)}, f32[128,4096]{1,0:T(8,128)}, f32[64,4096]{1,0:T(8,128)}, bf16[64,4096]{1,0:T(8,128)(2,1)}, s32[128]{0:T(128)S(1)}, /*index=5*/bf16[...) while((s32[]{:T(128)}, f32[128,4096]{1,0:T(8,128)}, ...), condition=%wide.region_1.2_spmd.clone.clone, body=%wide.region_0.1_spmd.clone.sunk.clone | while | flops 34604080 | bytes 66786340 | solution.py:47
  39.9 19.0 %while.22 = (s32[]{:T(128)}, bf16[256,4096]{1,0:T(8,128)(2,1)S(1)}, s32[8,2]{0,1:T(2,128)S(1)}, bf16[8,128,4096]{2,1,0:T(8,128)(2,1)}, s32[]{:T(128)}) while((s32[]{:T(128)}, bf16[256,4096]{1,0:T(8,128)(2,1)S(1)}, s32[8,2]{0,1:T(2,128)S(1)}, bf16[8,128,4096]{2,1,0:T(8,128)(2,1)}, s32[]{:T(128)}) %tuple.56), condition=%wide.while_cond, body=%wide.while_body.sunk | while | flops 2 | bytes 2098265 | solution.py:30
  42.8 1.8 bitcast_dynamic-update-slice_fusion.5
  45.2 1.8 bitcast_dynamic-update-slice_fusion.5
  52.3 1.8 bitcast_dynamic-update-slice_fusion.5
  54.7 1.8 bitcast_dynamic-update-slice_fusion.5
  59.0 8.2 %multiply_reduce_fusion.6 = f32[4096,128]{0,1:T(8,128)} fusion(f32[4096,8]{0,1:T(8,128)S(1)} %bitcast_convert_fusion.6, bf16[8,128,4096]{2,1,0:T(8,128)(2,1)} %get-tuple-element.289, pred[8,128]{1,0:T(8,128)(4,1)S(1)} %broadcast_compare_fusion.3), kind=kLoop, calls=%fused_computation.4.clone.1.clone | loop fusion | flops 16252928 | bytes 10617856 | tf_op jit(solution)/shard_map/while/body/eval_jaxpr/trc,tc->rc/dot_general | solution.py:36
  67.1 3.4 bitcast_add_fusion.3
  71.9 3.7 multiply_reduce_fusion.7
  77.1 19.0 %while.22 = (s32[]{:T(128)}, bf16[256,4096]{1,0:T(8,128)(2,1)S(1)}, s32[8,2]{0,1:T(2,128)S(1)}, bf16[8,128,4096]{2,1,0:T(8,128)(2,1)}, s32[]{:T(128)}) while((s32[]{:T(128)}, bf16[256,4096]{1,0:T(8,128)(2,1)S(1)}, s32[8,2]{0,1:T(2,128)S(1)}, bf16[8,128,4096]{2,1,0:T(8,128)(2,1)}, s32[]{:T(128)}) %tuple.56), condition=%wide.while_cond, body=%wide.while_body.sunk | while | flops 2 | bytes 2098265 | solution.py:30
  80.1 1.8 bitcast_dynamic-update-slice_fusion.5
  82.5 1.8 bitcast_dynamic-update-slice_fusion.5
  89.6 1.8 bitcast_dynamic-update-slice_fusion.5
  91.9 1.8 bitcast_dynamic-update-slice_fusion.5
  96.2 8.2 %multiply_reduce_fusion.6 = f32[4096,128]{0,1:T(8,128)} fusion(f32[4096,8]{0,1:T(8,128)S(1)} %bitcast_convert_fusion.6, bf16[8,128,4096]{2,1,0:T(8,128)(2,1)} %get-tuple-element.289, pred[8,128]{1,0:T(8,128)(4,1)S(1)} %broadcast_compare_fusion.3), kind=kLoop, calls=%fused_computation.4.clone.1.clone | loop fusion | flops 16252928 | bytes 10617856 | tf_op jit(solution)/shard_map/while/body/eval_jaxpr/trc,tc->rc/dot_general | solution.py:36
  104.4 4.0 bitcast_add_fusion.3
  109.8 3.7 multiply_reduce_fusion.7
  115.0 19.0 %while.22 = (s32[]{:T(128)}, bf16[256,4096]{1,0:T(8,128)(2,1)S(1)}, s32[8,2]{0,1:T(2,128)S(1)}, bf16[8,128,4096]{2,1,0:T(8,128)(2,1)}, s32[]{:T(128)}) while((s32[]{:T(128)}, bf16[256,4096]{1,0:T(8,128)(2,1)S(1)}, s32[8,2]{0,1:T(2,128)S(1)}, bf16[8,128,4096]{2,1,0:T(8,128)(2,1)}, s32[]{:T(128)}) %tuple.56), condition=%wide.while_cond, body=%wide.while_body.sunk | while | flops 2 | bytes 2098265 | solution.py:30
  118.0 1.8 bitcast_dynamic-update-slice_fusion.5
  127.4 1.8 bitcast_dynamic-update-slice_fusion.5
  129.8 1.8 bitcast_dynamic-update-slice_fusion.5
  134.1 8.2 %multiply_reduce_fusion.6 = f32[4096,128]{0,1:T(8,128)} fusion(f32[4096,8]{0,1:T(8,128)S(1)} %bitcast_convert_fusion.6, bf16[8,128,4096]{2,1,0:T(8,128)(2,1)} %get-tuple-element.289, pred[8,128]{1,0:T(8,128)(4,1)S(1)} %broadcast_compare_fusion.3), kind=kLoop, calls=%fused_computation.4.clone.1.clone | loop fusion | flops 16252928 | bytes 10617856 | tf_op jit(solution)/shard_map/while/body/eval_jaxpr/trc,tc->rc/dot_general | solution.py:36
  142.2 4.0 bitcast_add_fusion.3
  147.6 3.7 multiply_reduce_fusion.7
  152.9 19.0 %while.22 = (s32[]{:T(128)}, bf16[256,4096]{1,0:T(8,128)(2,1)S(1)}, s32[8,2]{0,1:T(2,128)S(1)}, bf16[8,128,4096]{2,1,0:T(8,128)(2,1)}, s32[]{:T(128)}) while((s32[]{:T(128)}, bf16[256,4096]{1,0:T(8,128)(2,1)S(1)}, s32[8,2]{0,1:T(2,128)S(1)}, bf16[8,128,4096]{2,1,0:T(8,128)(2,1)}, s32[]{:T(128)}) %tuple.56), condition=%wide.while_cond, body=%wide.while_body.sunk | while | flops 2 | bytes 2098265 | solution.py:30
  155.8 1.8 bitcast_dynamic-update-slice_fusion.5
  165.3 1.8 bitcast_dynamic-update-slice_fusion.5
  167.7 1.8 bitcast_dynamic-update-slice_fusion.5
  172.0 8.2 %multiply_reduce_fusion.6 = f32[4096,128]{0,1:T(8,128)} fusion(f32[4096,8]{0,1:T(8,128)S(1)} %bitcast_convert_fusion.6, bf16[8,128,4096]{2,1,0:T(8,128)(2,1)} %get-tuple-element.289, pred[8,128]{1,0:T(8,128)(4,1)S(1)} %broadcast_compare_fusion.3), kind=kLoop, calls=%fused_computation.4.clone.1.clone | loop fusion | flops 16252928 | bytes 10617856 | tf_op jit(solution)/shard_map/while/body/eval_jaxpr/trc,tc->rc/dot_general | solution.py:36
  180.1 4.0 bitcast_add_fusion.3
  185.5 3.7 multiply_reduce_fusion.7
  190.8 19.0 %while.22 = (s32[]{:T(128)}, bf16[256,4096]{1,0:T(8,128)(2,1)S(1)}, s32[8,2]{0,1:T(2,128)S(1)}, bf16[8,128,4096]{2,1,0:T(8,128)(2,1)}, s32[]{:T(128)}) while((s32[]{:T(128)}, bf16[256,4096]{1,0:T(8,128)(2,1)S(1)}, s32[8,2]{0,1:T(2,128)S(1)}, bf16[8,128,4096]{2,1,0:T(8,128)(2,1)}, s32[]{:T(128)}) %tuple.56), condition=%wide.while_cond, body=%wide.while_body.sunk | while | flops 2 | bytes 2098265 | solution.py:30
  193.7 1.8 bitcast_dynamic-update-slice_fusion.5
  203.2 1.8 bitcast_dynamic-update-slice_fusion.5
  205.6 1.8 bitcast_dynamic-update-slice_fusion.5
  209.8 8.2 %multiply_reduce_fusion.6 = f32[4096,128]{0,1:T(8,128)} fusion(f32[4096,8]{0,1:T(8,128)S(1)} %bitcast_convert_fusion.6, bf16[8,128,4096]{2,1,0:T(8,128)(2,1)} %get-tuple-element.289, pred[8,128]{1,0:T(8,128)(4,1)S(1)} %broadcast_compare_fusion.3), kind=kLoop, calls=%fused_computation.4.clone.1.clone | loop fusion | flops 16252928 | bytes 10617856 | tf_op jit(solution)/shard_map/while/body/eval_jaxpr/trc,tc->rc/dot_general | solution.py:36
  218.0 4.0 bitcast_add_fusion.3
  223.4 3.7 multiply_reduce_fusion.7
  228.7 19.0 %while.22 = (s32[]{:T(128)}, bf16[256,4096]{1,0:T(8,128)(2,1)S(1)}, s32[8,2]{0,1:T(2,128)S(1)}, bf16[8,128,4096]{2,1,0:T(8,128)(2,1)}, s32[]{:T(128)}) while((s32[]{:T(128)}, bf16[256,4096]{1,0:T(8,128)(2,1)S(1)}, s32[8,2]{0,1:T(2,128)S(1)}, bf16[8,128,4096]{2,1,0:T(8,128)(2,1)}, s32[]{:T(128)}) %tuple.56), condition=%wide.while_cond, body=%wide.while_body.sunk | while | flops 2 | bytes 2098265 | solution.py:30
  231.6 1.8 bitcast_dynamic-update-slice_fusion.5
  241.1 1.8 bitcast_dynamic-update-slice_fusion.5
  243.5 1.8 bitcast_dynamic-update-slice_fusion.5
  247.7 8.2 %multiply_reduce_fusion.6 = f32[4096,128]{0,1:T(8,128)} fusion(f32[4096,8]{0,1:T(8,128)S(1)} %bitcast_convert_fusion.6, bf16[8,128,4096]{2,1,0:T(8,128)(2,1)} %get-tuple-element.289, pred[8,128]{1,0:T(8,128)(4,1)S(1)} %broadcast_compare_fusion.3), kind=kLoop, calls=%fused_computation.4.clone.1.clone | loop fusion | flops 16252928 | bytes 10617856 | tf_op jit(solution)/shard_map/while/body/eval_jaxpr/trc,tc->rc/dot_general | solution.py:36
  255.9 4.0 bitcast_add_fusion.3
  261.3 3.7 multiply_reduce_fusion.7
  266.5 19.0 %while.22 = (s32[]{:T(128)}, bf16[256,4096]{1,0:T(8,128)(2,1)S(1)}, s32[8,2]{0,1:T(2,128)S(1)}, bf16[8,128,4096]{2,1,0:T(8,128)(2,1)}, s32[]{:T(128)}) while((s32[]{:T(128)}, bf16[256,4096]{1,0:T(8,128)(2,1)S(1)}, s32[8,2]{0,1:T(2,128)S(1)}, bf16[8,128,4096]{2,1,0:T(8,128)(2,1)}, s32[]{:T(128)}) %tuple.56), condition=%wide.while_cond, body=%wide.while_body.sunk | while | flops 2 | bytes 2098265 | solution.py:30
  269.5 1.8 bitcast_dynamic-update-slice_fusion.5
  278.9 1.8 bitcast_dynamic-update-slice_fusion.5
  281.3 1.8 bitcast_dynamic-update-slice_fusion.5
  285.6 8.2 %multiply_reduce_fusion.6 = f32[4096,128]{0,1:T(8,128)} fusion(f32[4096,8]{0,1:T(8,128)S(1)} %bitcast_convert_fusion.6, bf16[8,128,4096]{2,1,0:T(8,128)(2,1)} %get-tuple-element.289, pred[8,128]{1,0:T(8,128)(4,1)S(1)} %broadcast_compare_fusion.3), kind=kLoop, calls=%fused_computation.4.clone.1.clone | loop fusion | flops 16252928 | bytes 10617856 | tf_op jit(solution)/shard_map/while/body/eval_jaxpr/trc,tc->rc/dot_general | solution.py:36
  293.7 4.0 bitcast_add_fusion.3
  299.1 3.7 multiply_reduce_fusion.7
  304.4 19.0 %while.22 = (s32[]{:T(128)}, bf16[256,4096]{1,0:T(8,128)(2,1)S(1)}, s32[8,2]{0,1:T(2,128)S(1)}, bf16[8,128,4096]{2,1,0:T(8,128)(2,1)}, s32[]{:T(128)}) while((s32[]{:T(128)}, bf16[256,4096]{1,0:T(8,128)(2,1)S(1)}, s32[8,2]{0,1:T(2,128)S(1)}, bf16[8,128,4096]{2,1,0:T(8,128)(2,1)}, s32[]{:T(128)}) %tuple.56), condition=%wide.while_cond, body=%wide.while_body.sunk | while | flops 2 | bytes 2098265 | solution.py:30
  307.3 1.8 bitcast_dynamic-update-slice_fusion.5
  316.8 1.8 bitcast_dynamic-update-slice_fusion.5
  319.2 1.8 bitcast_dynamic-update-slice_fusion.5
  323.5 8.2 %multiply_reduce_fusion.6 = f32[4096,128]{0,1:T(8,128)} fusion(f32[4096,8]{0,1:T(8,128)S(1)} %bitcast_convert_fusion.6, bf16[8,128,4096]{2,1,0:T(8,128)(2,1)} %get-tuple-element.289, pred[8,128]{1,0:T(8,128)(4,1)S(1)} %broadcast_compare_fusion.3), kind=kLoop, calls=%fused_computation.4.clone.1.clone | loop fusion | flops 16252928 | bytes 10617856 | tf_op jit(solution)/shard_map/while/body/eval_jaxpr/trc,tc->rc/dot_general | solution.py:36
  331.6 4.0 bitcast_add_fusion.3
  337.0 3.7 multiply_reduce_fusion.7
  341.5 70.3 %reduce-scatter.2.cloned.1.call-done = f32[256,64]{0,1:T(8,128)} async-done(((f32[4096,64]{0,1:T(8,128)}), f32[256,64]{0,1:T(8,128)}) %reduce-scatter.2.cloned.1.call-update) | async-done | bytes 65552 | tf_op jit(solution)/shard_map/reduce_scatter | solution.py:50
  411.8 2.7 convert_element_type.15
  414.5 273.6 %all-reduce.3.cloned.1.call-done = f32[256,64]{0,1:T(8,128)} async-done(((f32[256,64]{0,1:T(8,128)}), f32[256,64]{0,1:T(8,128)}) %all-reduce.3.cloned.1.call-update) | async-done | bytes 65552 | tf_op jit(solution)/shard_map/psum | solution.py:51
  (261 shorter events, 134.6 us)
Async XLA Ops:
  7.2 31.8 %copy-start.1 = (bf16[128,4096]{1,0:T(8,128)(2,1)S(1)}, bf16[128,4096]{1,0:T(8,128)(2,1)}, u32[]{:S(2)}) copy-start(bf16[128,4096]{1,0:T(8,128)(2,1)} %param.9) | copy-start | bytes 3145732
  7.2 404.6 %reduce-scatter.2.cloned.1.call-start = ((), (), s32[]{:S(2)}) async-start(), calls=%async_computation.1 | async-start | bytes 1114112 | tf_op jit(solution)/shard_map/reduce_scatter | solution.py:50
  9.1 26.8 %copy-start.2 = (bf16[128,4096]{1,0:T(8,128)(2,1)}, bf16[128,4096]{1,0:T(8,128)(2,1)S(1)}, u32[]{:S(2)}) copy-start(bf16[128,4096]{1,0:T(8,128)(2,1)S(1)} %multiply_convert_fusion) | copy-start | bytes 3145732
  9.1 27.1 %collective-permute-start = (bf16[128,4096]{1,0:T(8,128)(2,1)S(1)}, bf16[128,4096]{1,0:T(8,128)(2,1)}, u32[]{:S(2)}, u32[]{:S(2)}) collective-permute-start(bf16[128,4096]{1,0:T(8,128)(2,1)S(1)} %multiply_convert_fusion), channel_id=1, source_target_pairs={{1,0},{2,1},{3,2},{4,3},{5,4},{6,5},{7,6},{8,7},{9,8},{10,9},{11,1... | collective-permute-start | bytes 3145736 | tf_op jit(solution)/shard_map/ppermute | solution.py:10
  67.1 4.8 copy-start
  104.4 5.4 copy-start
  142.2 5.4 copy-start
  180.1 5.4 copy-start
  218.0 5.4 copy-start
  255.9 5.4 copy-start
  293.7 5.4 copy-start
  331.6 5.4 copy-start
  341.4 346.7 %all-reduce.3.cloned.1.call-start = ((), (), s32[]{:S(2)}) async-start(), calls=%async_computation.2 | async-start | bytes 131072 | tf_op jit(solution)/shard_map/psum | solution.py:51
Sparse Core Ops, SparseCore 0:
  341.6 70.2 reduce-scatter.1
  414.7 273.3 all-reduce.2
where the time goes:
time: 698 us; the launch traced here: 696 us
  waiting for transfers between devices  344 us (49%)
  local copies, waits for them, and re-layouts  169 us (24%)
  other arithmetic  142 us (20%)
  blocking collectives  24.8 us (4%)
  between operations  14.1 us (2%)
    psum x1, waiting for transfers between devices, body(): grad_filt = lax.psum(owned, 'ctx')  274 us
    gather x192, local copies, waits for them, and re-layouts  152 us
    reduce_scatter x1, waiting for transfers between devices, body(): owned = lax.psum_scatter(filt_terms, 'dp', scatter_dimension=0, tiled=True)  70.3 us
    dot_general x8, other arithmetic, one_group(): jnp.einsum('trc,tc->rc', windows, weights, preferred_element_type=jnp.flo...  65.2 us
    add x8, other arithmetic, one_group(): accum + jnp.einsum('trc,tc->rc', windows, weights, preferred_element_type...  31.5 us
    dot_general x8, other arithmetic, one_group(): jnp.einsum('trc,rc->tc', windows, conv_in, preferred_element_type=jnp.flo...  29.6 us
    all_gather x1, blocking collectives, body(): whole_filter = lax.all_gather(filt, 'dp', axis=0, tiled=True)  24.8 us
  transfers between devices with their start and end apart: 3, of which 3 were waited for; matrix products, arithmetic and copies ran while one was open for 0% of the time, Pallas kernels for 0%

commit v1 on v0

--- a/solution.py
+++ b/solution.py
@@ -48,7 +48,7 @@
     grad_in = accum.astype(jnp.bfloat16)
     filt_terms = tap_rows.T
     owned = lax.psum_scatter(filt_terms, "dp", scatter_dimension=0, tiled=True)
-    grad_filt = lax.psum(owned, "ctx")
+    grad_filt = jnp.sum(lax.all_gather(owned, "ctx"), axis=0)
     return (grad_in, grad_filt)
 
 

time: 698 us -> 581 us (0.83)
  waiting for transfers between devices: 344 us -> 220 us
  local copies, waits for them, and re-layouts: 169 us -> 177 us
    psum x1 -> x0, waiting for transfers between devices: 274 us -> none  [body(): grad_filt = lax.psum(owned, 'ctx')]
    all_gather x0 -> x1, waiting for transfers between devices: none -> 148 us  [body(): grad_filt = jnp.sum(lax.all_gather(owned, 'ctx'), axis=0)]
    gather x192, local copies, waits for them, and re-layouts: 152 us -> 159 us
where the time goes in v1:
time: 581 us; the launch traced here: 580 us
  waiting for transfers between devices  220 us (38%)
  local copies, waits for them, and re-layouts  177 us (30%)
  other arithmetic  142 us (24%)
  blocking collectives  24.6 us (4%)
  between operations  14.1 us (2%)
    gather x192, local copies, waits for them, and re-layouts  159 us
    all_gather x1, waiting for transfers between devices, body(): grad_filt = jnp.sum(lax.all_gather(owned, 'ctx'), axis=0)  148 us
    reduce_scatter x1, waiting for transfers between devices, body(): owned = lax.psum_scatter(filt_terms, 'dp', scatter_dimension=0, tiled=True)  70.3 us
    dot_general x8, other arithmetic, one_group(): jnp.einsum('trc,tc->rc', windows, weights, preferred_element_type=jnp.flo...  65.1 us
    add x8, other arithmetic, one_group(): accum + jnp.einsum('trc,tc->rc', windows, weights, preferred_element_type...  31.4 us
    dot_general x8, other arithmetic, one_group(): jnp.einsum('trc,rc->tc', windows, conv_in, preferred_element_type=jnp.flo...  29.6 us
    all_gather x1, blocking collectives, body(): whole_filter = lax.all_gather(filt, 'dp', axis=0, tiled=True)  24.6 us
  transfers between devices with their start and end apart: 3, of which 3 were waited for; matrix products, arithmetic and copies ran while one was open for 0% of the time, Pallas kernels for 0%

profile of v1, /device:TPU:2, one launch (start us, length us, event | category | flops | bytes accessed | tf_op | source)
XLA Modules:
  0.0 579.8 jit_solution(4671298939726447994)
XLA Ops:
  10.4 24.6 %all_gather.9 = bf16[4096,64]{0,1:T(8,128)(2,1)} all-gather(bf16[256,64]{0,1:T(8,128)(2,1)S(1)} %copy-done.3), channel_id=1, replica_groups=mesh['dp'=16,'ctx'=32] {'dp'}, dimensions={0}, use_global_device_ids=true | all-gather | bytes 557056 | tf_op jit(solution)/shard_map/all_gather | solution.py:17
  38.9 309.9 %while.23 = (s32[]{:T(128)}, f32[128,4096]{1,0:T(8,128)}, f32[64,4096]{1,0:T(8,128)}, bf16[64,4096]{1,0:T(8,128)(2,1)}, s32[128]{0:T(128)S(1)}, /*index=5*/bf16[...) while((s32[]{:T(128)}, f32[128,4096]{1,0:T(8,128)}, ...), condition=%wide.region_1.2_spmd.clone.clone, body=%wide.region_0.1_spmd.clone.sunk.clone | while | flops 34604080 | bytes 66786340 | solution.py:47
  39.7 19.9 %while.22 = (s32[]{:T(128)}, bf16[256,4096]{1,0:T(8,128)(2,1)S(1)}, s32[8,2]{0,1:T(2,128)S(1)}, bf16[8,128,4096]{2,1,0:T(8,128)(2,1)}, s32[]{:T(128)}) while((s32[]{:T(128)}, bf16[256,4096]{1,0:T(8,128)(2,1)S(1)}, s32[8,2]{0,1:T(2,128)S(1)}, bf16[8,128,4096]{2,1,0:T(8,128)(2,1)}, s32[]{:T(128)}) %tuple.56), condition=%wide.while_cond, body=%wide.while_body.sunk | while | flops 2 | bytes 2098265 | solution.py:30
  42.9 1.9 bitcast_dynamic-update-slice_fusion.5
  52.8 1.9 bitcast_dynamic-update-slice_fusion.5
  55.3 1.9 bitcast_dynamic-update-slice_fusion.5
  59.8 8.1 %multiply_reduce_fusion.6 = f32[4096,128]{0,1:T(8,128)} fusion(f32[4096,8]{0,1:T(8,128)S(1)} %bitcast_convert_fusion.6, bf16[8,128,4096]{2,1,0:T(8,128)(2,1)} %get-tuple-element.289, pred[8,128]{1,0:T(8,128)(4,1)S(1)} %broadcast_compare_fusion.3), kind=kLoop, calls=%fused_computation.4.clone.1.clone | loop fusion | flops 16252928 | bytes 10617856 | tf_op jit(solution)/shard_map/while/body/eval_jaxpr/trc,tc->rc/dot_general | solution.py:36
  67.9 3.4 bitcast_add_fusion.3
  72.7 3.7 multiply_reduce_fusion.7
  77.9 19.9 %while.22 = (s32[]{:T(128)}, bf16[256,4096]{1,0:T(8,128)(2,1)S(1)}, s32[8,2]{0,1:T(2,128)S(1)}, bf16[8,128,4096]{2,1,0:T(8,128)(2,1)}, s32[]{:T(128)}) while((s32[]{:T(128)}, bf16[256,4096]{1,0:T(8,128)(2,1)S(1)}, s32[8,2]{0,1:T(2,128)S(1)}, bf16[8,128,4096]{2,1,0:T(8,128)(2,1)}, s32[]{:T(128)}) %tuple.56), condition=%wide.while_cond, body=%wide.while_body.sunk | while | flops 2 | bytes 2098265 | solution.py:30
  81.0 1.9 bitcast_dynamic-update-slice_fusion.5
  83.5 1.9 bitcast_dynamic-update-slice_fusion.5
  91.0 1.9 bitcast_dynamic-update-slice_fusion.5
  97.9 8.1 %multiply_reduce_fusion.6 = f32[4096,128]{0,1:T(8,128)} fusion(f32[4096,8]{0,1:T(8,128)S(1)} %bitcast_convert_fusion.6, bf16[8,128,4096]{2,1,0:T(8,128)(2,1)} %get-tuple-element.289, pred[8,128]{1,0:T(8,128)(4,1)S(1)} %broadcast_compare_fusion.3), kind=kLoop, calls=%fused_computation.4.clone.1.clone | loop fusion | flops 16252928 | bytes 10617856 | tf_op jit(solution)/shard_map/while/body/eval_jaxpr/trc,tc->rc/dot_general | solution.py:36
  106.1 4.0 bitcast_add_fusion.3
  111.5 3.7 multiply_reduce_fusion.7
  116.7 19.9 %while.22 = (s32[]{:T(128)}, bf16[256,4096]{1,0:T(8,128)(2,1)S(1)}, s32[8,2]{0,1:T(2,128)S(1)}, bf16[8,128,4096]{2,1,0:T(8,128)(2,1)}, s32[]{:T(128)}) while((s32[]{:T(128)}, bf16[256,4096]{1,0:T(8,128)(2,1)S(1)}, s32[8,2]{0,1:T(2,128)S(1)}, bf16[8,128,4096]{2,1,0:T(8,128)(2,1)}, s32[]{:T(128)}) %tuple.56), condition=%wide.while_cond, body=%wide.while_body.sunk | while | flops 2 | bytes 2098265 | solution.py:30
  119.8 1.9 bitcast_dynamic-update-slice_fusion.5
  122.4 1.9 bitcast_dynamic-update-slice_fusion.5
  129.8 1.9 bitcast_dynamic-update-slice_fusion.5
  132.3 1.9 bitcast_dynamic-update-slice_fusion.5
  136.7 8.1 %multiply_reduce_fusion.6 = f32[4096,128]{0,1:T(8,128)} fusion(f32[4096,8]{0,1:T(8,128)S(1)} %bitcast_convert_fusion.6, bf16[8,128,4096]{2,1,0:T(8,128)(2,1)} %get-tuple-element.289, pred[8,128]{1,0:T(8,128)(4,1)S(1)} %broadcast_compare_fusion.3), kind=kLoop, calls=%fused_computation.4.clone.1.clone | loop fusion | flops 16252928 | bytes 10617856 | tf_op jit(solution)/shard_map/while/body/eval_jaxpr/trc,tc->rc/dot_general | solution.py:36
  144.9 4.0 bitcast_add_fusion.3
  150.3 3.7 multiply_reduce_fusion.7
  155.6 19.9 %while.22 = (s32[]{:T(128)}, bf16[256,4096]{1,0:T(8,128)(2,1)S(1)}, s32[8,2]{0,1:T(2,128)S(1)}, bf16[8,128,4096]{2,1,0:T(8,128)(2,1)}, s32[]{:T(128)}) while((s32[]{:T(128)}, bf16[256,4096]{1,0:T(8,128)(2,1)S(1)}, s32[8,2]{0,1:T(2,128)S(1)}, bf16[8,128,4096]{2,1,0:T(8,128)(2,1)}, s32[]{:T(128)}) %tuple.56), condition=%wide.while_cond, body=%wide.while_body.sunk | while | flops 2 | bytes 2098265 | solution.py:30
  158.7 1.9 bitcast_dynamic-update-slice_fusion.5
  161.2 1.9 bitcast_dynamic-update-slice_fusion.5
  175.6 8.1 %multiply_reduce_fusion.6 = f32[4096,128]{0,1:T(8,128)} fusion(f32[4096,8]{0,1:T(8,128)S(1)} %bitcast_convert_fusion.6, bf16[8,128,4096]{2,1,0:T(8,128)(2,1)} %get-tuple-element.289, pred[8,128]{1,0:T(8,128)(4,1)S(1)} %broadcast_compare_fusion.3), kind=kLoop, calls=%fused_computation.4.clone.1.clone | loop fusion | flops 16252928 | bytes 10617856 | tf_op jit(solution)/shard_map/while/body/eval_jaxpr/trc,tc->rc/dot_general | solution.py:36
  183.7 4.0 bitcast_add_fusion.3
  189.1 3.7 multiply_reduce_fusion.7
  194.4 19.9 %while.22 = (s32[]{:T(128)}, bf16[256,4096]{1,0:T(8,128)(2,1)S(1)}, s32[8,2]{0,1:T(2,128)S(1)}, bf16[8,128,4096]{2,1,0:T(8,128)(2,1)}, s32[]{:T(128)}) while((s32[]{:T(128)}, bf16[256,4096]{1,0:T(8,128)(2,1)S(1)}, s32[8,2]{0,1:T(2,128)S(1)}, bf16[8,128,4096]{2,1,0:T(8,128)(2,1)}, s32[]{:T(128)}) %tuple.56), condition=%wide.while_cond, body=%wide.while_body.sunk | while | flops 2 | bytes 2098265 | solution.py:30
  197.5 1.9 bitcast_dynamic-update-slice_fusion.5
  207.4 1.9 bitcast_dynamic-update-slice_fusion.5
  209.9 1.9 bitcast_dynamic-update-slice_fusion.5
  214.4 8.1 %multiply_reduce_fusion.6 = f32[4096,128]{0,1:T(8,128)} fusion(f32[4096,8]{0,1:T(8,128)S(1)} %bitcast_convert_fusion.6, bf16[8,128,4096]{2,1,0:T(8,128)(2,1)} %get-tuple-element.289, pred[8,128]{1,0:T(8,128)(4,1)S(1)} %broadcast_compare_fusion.3), kind=kLoop, calls=%fused_computation.4.clone.1.clone | loop fusion | flops 16252928 | bytes 10617856 | tf_op jit(solution)/shard_map/while/body/eval_jaxpr/trc,tc->rc/dot_general | solution.py:36
  222.5 4.0 bitcast_add_fusion.3
  227.9 3.7 multiply_reduce_fusion.7
  233.2 19.9 %while.22 = (s32[]{:T(128)}, bf16[256,4096]{1,0:T(8,128)(2,1)S(1)}, s32[8,2]{0,1:T(2,128)S(1)}, bf16[8,128,4096]{2,1,0:T(8,128)(2,1)}, s32[]{:T(128)}) while((s32[]{:T(128)}, bf16[256,4096]{1,0:T(8,128)(2,1)S(1)}, s32[8,2]{0,1:T(2,128)S(1)}, bf16[8,128,4096]{2,1,0:T(8,128)(2,1)}, s32[]{:T(128)}) %tuple.56), condition=%wide.while_cond, body=%wide.while_body.sunk | while | flops 2 | bytes 2098265 | solution.py:30
  236.3 1.9 bitcast_dynamic-update-slice_fusion.5
  238.8 1.9 bitcast_dynamic-update-slice_fusion.5
  246.2 1.9 bitcast_dynamic-update-slice_fusion.5
  248.7 1.9 bitcast_dynamic-update-slice_fusion.5
  253.2 8.1 %multiply_reduce_fusion.6 = f32[4096,128]{0,1:T(8,128)} fusion(f32[4096,8]{0,1:T(8,128)S(1)} %bitcast_convert_fusion.6, bf16[8,128,4096]{2,1,0:T(8,128)(2,1)} %get-tuple-element.289, pred[8,128]{1,0:T(8,128)(4,1)S(1)} %broadcast_compare_fusion.3), kind=kLoop, calls=%fused_computation.4.clone.1.clone | loop fusion | flops 16252928 | bytes 10617856 | tf_op jit(solution)/shard_map/while/body/eval_jaxpr/trc,tc->rc/dot_general | solution.py:36
  261.3 4.0 bitcast_add_fusion.3
  266.7 3.7 multiply_reduce_fusion.7
  272.0 19.9 %while.22 = (s32[]{:T(128)}, bf16[256,4096]{1,0:T(8,128)(2,1)S(1)}, s32[8,2]{0,1:T(2,128)S(1)}, bf16[8,128,4096]{2,1,0:T(8,128)(2,1)}, s32[]{:T(128)}) while((s32[]{:T(128)}, bf16[256,4096]{1,0:T(8,128)(2,1)S(1)}, s32[8,2]{0,1:T(2,128)S(1)}, bf16[8,128,4096]{2,1,0:T(8,128)(2,1)}, s32[]{:T(128)}) %tuple.56), condition=%wide.while_cond, body=%wide.while_body.sunk | while | flops 2 | bytes 2098265 | solution.py:30
  275.1 1.9 bitcast_dynamic-update-slice_fusion.5
  277.6 1.9 bitcast_dynamic-update-slice_fusion.5
  285.1 1.9 bitcast_dynamic-update-slice_fusion.5
  287.6 1.9 bitcast_dynamic-update-slice_fusion.5
  292.0 8.1 %multiply_reduce_fusion.6 = f32[4096,128]{0,1:T(8,128)} fusion(f32[4096,8]{0,1:T(8,128)S(1)} %bitcast_convert_fusion.6, bf16[8,128,4096]{2,1,0:T(8,128)(2,1)} %get-tuple-element.289, pred[8,128]{1,0:T(8,128)(4,1)S(1)} %broadcast_compare_fusion.3), kind=kLoop, calls=%fused_computation.4.clone.1.clone | loop fusion | flops 16252928 | bytes 10617856 | tf_op jit(solution)/shard_map/while/body/eval_jaxpr/trc,tc->rc/dot_general | solution.py:36
  300.1 4.0 bitcast_add_fusion.3
  305.5 3.7 multiply_reduce_fusion.7
  310.8 19.9 %while.22 = (s32[]{:T(128)}, bf16[256,4096]{1,0:T(8,128)(2,1)S(1)}, s32[8,2]{0,1:T(2,128)S(1)}, bf16[8,128,4096]{2,1,0:T(8,128)(2,1)}, s32[]{:T(128)}) while((s32[]{:T(128)}, bf16[256,4096]{1,0:T(8,128)(2,1)S(1)}, s32[8,2]{0,1:T(2,128)S(1)}, bf16[8,128,4096]{2,1,0:T(8,128)(2,1)}, s32[]{:T(128)}) %tuple.56), condition=%wide.while_cond, body=%wide.while_body.sunk | while | flops 2 | bytes 2098265 | solution.py:30
  313.9 1.9 bitcast_dynamic-update-slice_fusion.5
  316.4 1.9 bitcast_dynamic-update-slice_fusion.5
  323.9 1.9 bitcast_dynamic-update-slice_fusion.5
  330.8 8.1 %multiply_reduce_fusion.6 = f32[4096,128]{0,1:T(8,128)} fusion(f32[4096,8]{0,1:T(8,128)S(1)} %bitcast_convert_fusion.6, bf16[8,128,4096]{2,1,0:T(8,128)(2,1)} %get-tuple-element.289, pred[8,128]{1,0:T(8,128)(4,1)S(1)} %broadcast_compare_fusion.3), kind=kLoop, calls=%fused_computation.4.clone.1.clone | loop fusion | flops 16252928 | bytes 10617856 | tf_op jit(solution)/shard_map/while/body/eval_jaxpr/trc,tc->rc/dot_general | solution.py:36
  339.0 4.0 bitcast_add_fusion.3
  344.4 3.7 multiply_reduce_fusion.7
  348.8 70.3 %reduce-scatter.2.cloned.1.call-done = f32[256,64]{0,1:T(8,128)} async-done(((f32[4096,64]{0,1:T(8,128)}), f32[256,64]{0,1:T(8,128)}) %reduce-scatter.2.cloned.1.call-update) | async-done | bytes 65552 | tf_op jit(solution)/shard_map/reduce_scatter | solution.py:50
  419.1 2.7 convert_element_type.15
  421.8 148.1 %all-gather.3.cloned.1.call-done = f32[8192,64]{0,1:T(8,128)} async-done(((f32[256,64]{0,1:T(8,128)}), f32[8192,64]{0,1:T(8,128)}) %all-gather.3.cloned.1.call-update) | async-done | bytes 2097168 | tf_op jit(solution)/shard_map/all_gather | solution.py:51
  569.9 2.2 copy.23
  (266 shorter events, 142.1 us)
Async XLA Ops:
  7.2 3.2 copy-start.4
  7.2 3.2 copy-start.3
  7.2 411.9 %reduce-scatter.2.cloned.1.call-start = ((), (), s32[]{:S(2)}) async-start(), calls=%async_computation.1 | async-start | bytes 1114112 | tf_op jit(solution)/shard_map/reduce_scatter | solution.py:50
  9.0 26.0 %copy-start.2 = (bf16[128,4096]{1,0:T(8,128)(2,1)}, bf16[128,4096]{1,0:T(8,128)(2,1)S(1)}, u32[]{:S(2)}) copy-start(bf16[128,4096]{1,0:T(8,128)(2,1)S(1)} %multiply_convert_fusion) | copy-start | bytes 3145732
  9.0 27.1 %collective-permute-start = (bf16[128,4096]{1,0:T(8,128)(2,1)S(1)}, bf16[128,4096]{1,0:T(8,128)(2,1)}, u32[]{:S(2)}, u32[]{:S(2)}) collective-permute-start(bf16[128,4096]{1,0:T(8,128)(2,1)S(1)} %multiply_convert_fusion), channel_id=1, source_target_pairs={{1,0},{2,1},{3,2},{4,3},{5,4},{6,5},{7,6},{8,7},{9,8},{10,9},{11,1... | collective-permute-start | bytes 3145736 | tf_op jit(solution)/shard_map/ppermute | solution.py:10
  35.0 3.8 copy-start.1
  67.9 4.8 copy-start
  106.1 5.4 copy-start
  144.9 5.4 copy-start
  183.7 5.4 copy-start
  222.5 5.4 copy-start
  261.3 5.4 copy-start
  300.1 5.4 copy-start
  339.0 5.4 copy-start
  348.8 221.2 %all-gather.3.cloned.1.call-start = ((), (), s32[]{:S(2)}) async-start(), calls=%async_computation.2 | async-start | bytes 2162688 | tf_op jit(solution)/shard_map/all_gather | solution.py:51
Sparse Core Ops, SparseCore 0:
  348.9 70.1 reduce-scatter.1
  422.0 147.8 all-gather.2
